TPU v7x, 32 devices: a whole 2x2x4 slice. The times are simulated.
32 devices in a mesh: tm: 1, space: 32 (over z, y, x, core).
Axes of the slice: x: 2, y: 2, z: 4, core: 2. Of those that a mesh axis runs over, the one named last changes fastest.
Arguments:
- links: float32 [8, 3, 2, 3, 2, 110592], P('tm', None, None, None, None, 'space'), may hold values from -1 to 1, as said below
Outputs:
- new_links: float32 [8, 3, 2, 3, 2, 110592], P('tm', None, None, None, None, 'space')
- theta: float32 [], replicated
- deficit: float32 [8], P('tm')
Inputs may be any that keep to these rules, and one draw needn't show every extreme that they name: `links`: each link's two stored rows are orthonormal complex 3-vectors, the first two rows of a special unitary matrix.
All inputs are finite; a program needn't handle non-finite values.
Results may differ from a plain program's by a relative error of at most 0.00013.
Values sent between devices are 32-bit elements; how exact they have to be, the bound alone decides.
A program may use at most 128 MiB of HBM per device.

v0:
```python
import math
import jax
import jax.numpy as jnp
from jax import lax
from jax.sharding import PartitionSpec as P

EXTENT = 48
root_three = math.sqrt(3.0)
step_size = 0.08
top_momentum = 12.0
storage_offset = 1


def from_behind(block, axis, distance):
    devices = range(lax.axis_size(axis))
    route = [((i - distance) % len(devices), i) for i in devices]
    return lax.ppermute(block, axis, route)


def complex_mul(p, q):
    return (p[0] * q[0] - p[1] * q[1], p[0] * q[1] + p[1] * q[0])


def complex_add(p, q):
    return (p[0] + q[0], p[1] + q[1])


def complex_sub(p, q):
    return (p[0] - q[0], p[1] - q[1])


def complex_conj(p):
    return (p[0], -p[1])


def matrix_mul(left, right):
    rows_out = []
    for i in range(len(left)):
        entries = []
        for j in range(3):
            summed = complex_mul(left[i][0], right[0][j])
            for k in (1, 2):
                summed = complex_add(summed, complex_mul(left[i][k], right[k][j]))
            entries.append(summed)
        rows_out.append(entries)
    return rows_out


def dagger_of(matrix):
    return [[complex_conj(matrix[j][i]) for j in range(3)] for i in range(3)]


def cross_conj(row_one, row_two):
    row_three = []
    for k in range(3):
        a = complex_mul(row_one[(k + 1) % 3], row_two[(k + 2) % 3])
        b = complex_mul(row_one[(k + 2) % 3], row_two[(k + 1) % 3])
        row_three.append(complex_conj(complex_sub(a, b)))
    return row_three


def full_matrix(entry_of):
    row_one = [(entry_of(0, c, 0), entry_of(0, c, 1)) for c in range(3)]
    row_two = [(entry_of(1, c, 0), entry_of(1, c, 1)) for c in range(3)]
    return [row_one, row_two, cross_conj(row_one, row_two)]


def link_matrix(arr):
    return full_matrix(lambda r, c, p: arr[:, r, c, p])


def gradient_of(current, behind):
    gradient = []
    for i in range(3):
        entries = []
        for j in range(3):
            summed = complex_sub(behind[0][i][j], current[0][i][j])
            for d in (1, 2):
                summed = complex_add(summed, complex_sub(behind[d][i][j], current[d][i][j]))
            entries.append(summed)
        gradient.append(entries)
    return gradient


def algebra_of(gradient):
    return [
        gradient[0][1][1] + gradient[1][0][1],
        gradient[0][1][0] - gradient[1][0][0],
        gradient[0][0][1] - gradient[1][1][1],
        gradient[0][2][1] + gradient[2][0][1],
        gradient[0][2][0] - gradient[2][0][0],
        gradient[1][2][1] + gradient[2][1][1],
        gradient[1][2][0] - gradient[2][1][0],
        (gradient[0][0][1] + gradient[1][1][1] - 2.0 * gradient[2][2][1]) / root_three,
    ]


def rotation_of(algebra):
    half_step = 0.5 * step_size
    zeros_like = jnp.zeros_like(algebra[0])
    diag_zero = algebra[2] + algebra[7] / root_three
    diag_one = -algebra[2] + algebra[7] / root_three
    diag_two = -2.0 * algebra[7] / root_three
    hermitian = [
        [(diag_zero, zeros_like), (algebra[0], -algebra[1]), (algebra[3], -algebra[4])],
        [(algebra[0], algebra[1]), (diag_one, zeros_like), (algebra[5], -algebra[6])],
        [(algebra[3], algebra[4]), (algebra[5], algebra[6]), (diag_two, zeros_like)],
    ]
    generator = [[(-half_step * h[1], half_step * h[0]) for h in row] for row in hermitian]
    square = matrix_mul(generator[:2], generator)
    rows_two = []
    for i in range(2):
        entries = []
        for j in range(3):
            real_value = generator[i][j][0] + 0.5 * square[i][j][0]
            if i == j:
                real_value = real_value + 1.0
            entries.append((real_value, generator[i][j][1] + 0.5 * square[i][j][1]))
        rows_two.append(entries)
    length = jnp.sqrt(sum((p[0] * p[0] + p[1] * p[1] for p in rows_two[0])))
    row_one = [(p[0] / length, p[1] / length) for p in rows_two[0]]
    correlation = complex_mul(complex_conj(row_one[0]), rows_two[1][0])
    for k in (1, 2):
        correlation = complex_add(
            correlation, complex_mul(complex_conj(row_one[k]), rows_two[1][k])
        )
    row_two = [complex_sub(rows_two[1][k], complex_mul(correlation, row_one[k])) for k in range(3)]
    length = jnp.sqrt(sum((p[0] * p[0] + p[1] * p[1] for p in row_two)))
    row_two = [(p[0] / length, p[1] / length) for p in row_two]
    return [row_one, row_two, cross_conj(row_one, row_two)]


def two_rows(product, axis):
    return jnp.stack(
        [
            jnp.stack([jnp.stack(product[r][c], axis=axis) for c in range(3)], axis=axis)
            for r in range(2)
        ],
        axis=axis,
    )


def matrix_stack(matrix):
    return jnp.stack([jnp.stack([jnp.stack(matrix[i][j]) for j in range(3)]) for i in range(3)])


def matrix_from(stacked):
    return [[(stacked[i, j, 0], stacked[i, j, 1]) for j in range(3)] for i in range(3)]


def plane_step(values, einsum_form, cosine_table, sine_table, sign_value, pair_count):
    highest = lax.Precision.HIGHEST
    with_cos = jnp.einsum(einsum_form, values, cosine_table, precision=highest)
    with_sin = jnp.einsum(einsum_form, values, sine_table, precision=highest)
    dims_shape = with_cos.shape
    with_cos = with_cos.reshape(dims_shape[0], dims_shape[1], pair_count, 2, -1)
    with_sin = with_sin.reshape(dims_shape[0], dims_shape[1], pair_count, 2, -1)
    real_out = with_cos[:, :, :, 0] - sign_value * with_sin[:, :, :, 1]
    imag_out = with_cos[:, :, :, 1] + sign_value * with_sin[:, :, :, 0]
    return jnp.stack([real_out, imag_out], axis=3).reshape(dims_shape)


def body(links):
    highest = lax.Precision.HIGHEST
    extent = EXTENT
    slices = links.shape[0]
    local_sites = links.shape[-1]
    plane_size = extent * extent
    lower_width = (extent - 1) * extent
    rows_dev = local_sites // extent
    device = lax.axis_index("space")
    site_index = jnp.arange(local_sites, dtype=jnp.int32)
    xcoord = site_index % extent
    zcoord = (device * rows_dev + site_index // extent - storage_offset) % extent
    along_x = links[:, 0]
    along_y = links[:, 1]
    along_z = links[:, 2]
    below_piece = jnp.concatenate(
        [along_y[..., local_sites - plane_size :], along_z[..., local_sites - extent :]], axis=-1
    )
    from_below = from_behind(below_piece, "space", 1)
    from_above = from_behind(along_z[..., : plane_size - extent], "space", -1)
    behind_x = jnp.where(
        xcoord == 0, jnp.roll(along_x, -(extent - 1), axis=-1), jnp.roll(along_x, 1, axis=-1)
    )
    behind_y = jnp.concatenate(
        [from_below[..., :plane_size], along_y[..., : local_sites - plane_size]], axis=-1
    )
    near_z = jnp.concatenate(
        [from_below[..., plane_size:], along_z[..., : local_sites - extent]], axis=-1
    )
    wrap_z = jnp.concatenate([along_z[..., plane_size - extent :], from_above], axis=-1)
    behind_z = jnp.where(zcoord == 0, wrap_z, near_z)
    current = [link_matrix(along_x), link_matrix(along_y), link_matrix(along_z)]
    behind = [link_matrix(behind_x), link_matrix(behind_y), link_matrix(behind_z)]
    algebra = algebra_of(gradient_of(current, behind))
    theta_part = sum((jnp.sum(a * a) for a in algebra))
    theta_total = lax.psum(theta_part, ("tm", "space"))
    wave_number = jnp.arange(extent, dtype=jnp.int32)
    angle_table = (
        2.0
        * math.pi
        / extent
        * (wave_number[:, None] * wave_number[None, :] % extent).astype(jnp.float32)
    )
    cosine_table = jnp.cos(angle_table)
    sine_table = jnp.sin(angle_table)
    fields = jnp.stack(algebra).reshape(8, slices, rows_dev, extent)
    paired = fields.reshape(4, 2, slices, rows_dev, extent)
    even_part = paired[:, 0]
    odd_part = paired[:, 1]
    real_x = jnp.einsum("csqx,kx->qcks", even_part, cosine_table, precision=highest)
    real_x = real_x + jnp.einsum("csqx,kx->qcks", odd_part, sine_table, precision=highest)
    imag_x = jnp.einsum("csqx,kx->qcks", odd_part, cosine_table, precision=highest)
    imag_x = imag_x - jnp.einsum("csqx,kx->qcks", even_part, sine_table, precision=highest)
    packed = jnp.stack([real_x, imag_x], axis=3).reshape(rows_dev, 4 * extent * 2 * slices)
    planes = lax.all_to_all(packed, "space", split_axis=1, concat_axis=0, tiled=True)
    pair_count = planes.shape[1] // (2 * slices)
    planes = jnp.roll(planes, -storage_offset, axis=0)
    planes = planes.reshape(extent, extent, planes.shape[1])
    planes = plane_step(planes, "yzc,kz->ykc", cosine_table, sine_table, -1.0, pair_count)
    planes = plane_step(planes, "yzc,ky->kzc", cosine_table, sine_table, -1.0, pair_count)
    pair_kx = (device * pair_count + jnp.arange(pair_count, dtype=jnp.int32)) % extent
    wave_term = 4.0 * jnp.sin(math.pi * wave_number.astype(jnp.float32) / extent) ** 2
    wave_pair = 4.0 * jnp.sin(math.pi * pair_kx.astype(jnp.float32) / extent) ** 2
    momentum = wave_term[:, None, None] + wave_term[None, :, None] + wave_pair[None, None, :]
    zero_mode = (
        wave_number[:, None, None] + wave_number[None, :, None] + pair_kx[None, None, :] == 0
    )
    factor = jnp.where(
        zero_mode, 0.0, top_momentum / (extent**3 * jnp.where(zero_mode, 1.0, momentum))
    )
    planes = (
        planes.reshape(extent, extent, pair_count, 2 * slices) * factor[:, :, :, None]
    ).reshape(extent, extent, -1)
    planes = plane_step(planes, "yzc,kz->ykc", cosine_table, sine_table, 1.0, pair_count)
    planes = plane_step(planes, "yzc,ky->kzc", cosine_table, sine_table, 1.0, pair_count)
    planes = jnp.roll(planes.reshape(plane_size, -1), storage_offset, axis=0)
    returned = lax.all_to_all(planes, "space", split_axis=0, concat_axis=1, tiled=True)
    returned = returned.reshape(rows_dev, 4, extent, 2, slices)
    real_back = returned[:, :, :, 0]
    imag_back = returned[:, :, :, 1]
    even_smooth = jnp.einsum("qcks,kx->csqx", real_back, cosine_table, precision=highest)
    even_smooth = even_smooth - jnp.einsum(
        "qcks,kx->csqx", imag_back, sine_table, precision=highest
    )
    odd_smooth = jnp.einsum("qcks,kx->csqx", real_back, sine_table, precision=highest)
    odd_smooth = odd_smooth + jnp.einsum(
        "qcks,kx->csqx", imag_back, cosine_table, precision=highest
    )
    smooth = jnp.stack([even_smooth, odd_smooth], axis=1).reshape(8, slices, local_sites)
    rotation = rotation_of([smooth[a] for a in range(8)])
    stacked = matrix_stack(rotation)
    upper_rim = from_behind(stacked[..., :plane_size], "space", -1)
    lower_rim = from_behind(stacked[..., local_sites - lower_width :], "space", 1)
    wide_rot = matrix_from(jnp.concatenate([lower_rim, stacked, upper_rim], axis=-1))
    ahead_x = jax.tree.map(
        lambda a: jnp.where(
            xcoord == extent - 1, jnp.roll(a, extent - 1, axis=-1), jnp.roll(a, -1, axis=-1)
        ),
        rotation,
    )
    ahead_y = jax.tree.map(
        lambda a: a[..., lower_width + plane_size : lower_width + plane_size + local_sites],
        wide_rot,
    )
    ahead_z = jax.tree.map(
        lambda a: jnp.where(
            zcoord == extent - 1,
            a[..., :local_sites],
            a[..., lower_width + extent : lower_width + extent + local_sites],
        ),
        wide_rot,
    )
    ahead_all = [ahead_x, ahead_y, ahead_z]
    new_dirs = []
    deficit_part = jnp.zeros((slices,), jnp.float32)
    for d in range(3):
        product = matrix_mul(matrix_mul(rotation, current[d]), dagger_of(ahead_all[d]))
        deficit_part = deficit_part + jnp.sum(
            3.0 - product[0][0][0] - product[1][1][0] - product[2][2][0], axis=-1
        )
        new_dirs.append(two_rows(product, 1))
    new_links = jnp.stack(new_dirs, axis=1)
    deficit_total = lax.psum(deficit_part, "space")
    theta = theta_total / (slices * lax.axis_size("tm") * extent**3)
    deficit = deficit_total / extent**3
    return (new_links, theta, deficit)


def solution(mesh):
    placed = (P("tm", None, None, None, None, "space"),)
    return jax.shard_map(
        body,
        mesh=mesh,
        in_specs=placed,
        out_specs=(P("tm", None, None, None, None, "space"), P(), P("tm")),
        check_vma=False,
    )
```

profile of v0, /device:TPU:12, one launch (start us, length us, event | category | flops | bytes accessed | tf_op | source)
XLA Modules:
  0.0 409.1 jit_solution(4929725969459849419)
XLA Ops:
  0.6 3.5 fusion.979
  12.0 16.0 %collective-permute-done = f32[8,2,3,2,2352]{4,0,3,2,1:T(8,128)} collective-permute-done((f32[8,2,3,2,2352]{4,0,3,2,1:T(8,128)}, f32[8,2,3,2,2352]{4,0,3,2,1:T(8,128)}, u32[]{:S(2)}, u32[]{:S(2)}) %collective-permute-start) | collective-permute-done | bytes 903200 | tf_op jit(solution)/shard_map/ppermute | solution.py:17
  40.9 3.7 reshape_reshape.9
  44.6 4.7 %fusion.9 = f32[48,4,8,72]{3,0,2,1:T(8,128)S(1)} fusion(f32[4,2,8,72,48]{4,3,2,1,0:T(8,128)} %reshape_reshape.9), kind=kOutput, calls=%fused_computation.67 | convolution fusion | flops 63721728 | bytes 1622016 | tf_op jit(solution)/shard_map/csqx,kx->qcks/dot_general | solution.py:214
  49.3 4.6 %fusion.8 = f32[48,4,8,72]{3,0,2,1:T(8,128)S(1)} fusion(f32[4,2,8,72,48]{4,3,2,1,0:T(8,128)} %reshape_reshape.9), kind=kOutput, calls=%fused_computation.66 | convolution fusion | flops 63721728 | bytes 1622016 | tf_op jit(solution)/shard_map/csqx,kx->qcks/dot_general | solution.py:212
  53.9 3.3 fusion.2
  57.3 3.3 fusion.3
  65.3 6.8 %all-to-all-start = ((f32[72,32,96]{2,0,1:T(8,128)}), f32[72,32,96]{2,0,1:T(8,128)}, u32[]{:S(2)}, u32[]{:S(2)}) async-start(f32[72,32,96]{2,0,1:T(8,128)} %copy.286), calls=%async_computation | async-start | bytes 2359296 | tf_op jit(solution)/shard_map/all_to_all | solution.py:217
  76.8 22.8 %all-to-all-done = f32[72,32,96]{2,0,1:T(8,128)} async-done(((f32[72,32,96]{2,0,1:T(8,128)}), f32[72,32,96]{2,0,1:T(8,128)}, u32[]{:S(2)}, u32[]{:S(2)}) %all-to-all-start) | async-done | bytes 884768 | tf_op jit(solution)/shard_map/all_to_all | solution.py:217
  116.4 3.1 copy.295
  119.5 10.3 %fusion.728 = f32[48,48,6,2,8]{1,0,4,3,2:T(8,128)S(1)} fusion(f32[48,6,2,8,48]{4,0,3,2,1:T(8,128)} %bitcast.4454), kind=kOutput, calls=%fused_computation.1642 | convolution fusion | flops 127422720 | bytes 1769472 | tf_op jit(solution)/shard_map/yzc,ky->kzc/dot_general | solution.py:154
  129.8 8.5 %fusion.738 = f32[48,48,6,2,8]{1,0,4,3,2:T(8,128)S(1)} fusion(f32[48,6,2,8,48]{4,0,3,2,1:T(8,128)S(1)} %bitcast.4455), kind=kOutput, calls=%fused_computation.1652 | convolution fusion | flops 127422720 | bytes 1769472 | tf_op jit(solution)/shard_map/yzc,ky->kzc/dot_general | solution.py:153
  140.2 3.2 copy.299
  143.4 4.1 convolution_bitcast_fusion
  159.8 3.2 copy.305
  163.0 10.3 %fusion.726 = f32[48,48,6,2,8]{1,0,4,3,2:T(8,128)S(1)} fusion(f32[48,6,2,8,48]{4,0,3,2,1:T(8,128)} %bitcast.4456), kind=kOutput, calls=%fused_computation.1640 | convolution fusion | flops 127422720 | bytes 1769472 | tf_op jit(solution)/shard_map/yzc,ky->kzc/dot_general | solution.py:154
  173.4 8.5 %fusion.740 = f32[48,48,6,2,8]{1,0,4,3,2:T(8,128)S(1)} fusion(f32[48,6,2,8,48]{4,0,3,2,1:T(8,128)S(1)} %bitcast.4457), kind=kOutput, calls=%fused_computation.1654 | convolution fusion | flops 127422720 | bytes 1769472 | tf_op jit(solution)/shard_map/yzc,ky->kzc/dot_general | solution.py:153
  191.6 5.0 %all-to-all-start.1 = ((f32[32,72,96]{2,1,0:T(8,128)}), f32[32,72,96]{2,1,0:T(8,128)}, u32[]{:S(2)}, u32[]{:S(2)}) async-start(f32[32,72,96]{2,1,0:T(8,128)} %bitcast.4470), calls=%async_computation.1 | async-start | bytes 2359296 | tf_op jit(solution)/shard_map/all_to_all | solution.py:239
  198.5 25.8 %all-to-all-done.1 = f32[32,72,96]{2,1,0:T(8,128)} async-done(((f32[32,72,96]{2,1,0:T(8,128)}), f32[32,72,96]{2,1,0:T(8,128)}, u32[]{:S(2)}, u32[]{:S(2)}) %all-to-all-start.1) | async-done | bytes 884768 | tf_op jit(solution)/shard_map/all_to_all | solution.py:239
  258.4 25.5 %collective-permute-done.2 = f32[3,3,2,8,2256]{4,3,2,1,0:T(8,128)} collective-permute-done((f32[3,3,2,8,2256]{4,3,2,1,0:T(8,128)S(1)}, f32[3,3,2,8,2256]{4,3,2,1,0:T(8,128)}, u32[]{:S(2)}, u32[]{:S(2)}) %collective-permute-start.2) | collective-permute-done | bytes 1299488 | tf_op jit(solution)/shard_map/ppermute | solution.py:17
  283.9 6.6 %concatenate.1157 = f32[3,3,2,8,8016]{4,3,2,1,0:T(8,128)} concatenate(f32[3,3,2,8,2256]{4,3,2,1,0:T(8,128)} %collective-permute-done.2, f32[3,3,2,8,3456]{4,3,2,1,0:T(8,128)} %copy-done.7, f32[3,3,2,8,2304]{4,3,2,1,0:T(8,128)} %collective-permute-done.3), dimensions={4} | concatenate | bytes 9234432 | tf_op jit(solution)/shard_map/concatenate | solution.py:256
  357.7 3.4 fusion.708
  361.7 4.0 copy.332
  365.7 40.9 %all-reduce = (f32[]{:T(128)}, f32[8]{0:T(128)S(1)}) all-reduce(f32[]{:T(128)S(6)} %add.9190, f32[8]{0:T(128)S(1)} %add_add_fusion.11), channel_id=1, replica_groups=mesh['tm'=1,'space'=32] {'tm','space'}, use_global_device_ids=true, to_apply=%region_8.9 | all-reduce | flops 9 | bytes 72 | tf_op jit(solution)/shard_map/psum | solution.py:198
  (466 shorter events, 168.5 us)
Async XLA Ops:
  5.2 24.8 %collective-permute-start.1 = (f32[8,2,3,2,2256]{4,0,3,2,1:T(8,128)}, f32[8,2,3,2,2256]{4,0,3,2,1:T(8,128)}, u32[]{:S(2)}, u32[]{:S(2)}) collective-permute-start(f32[8,2,3,2,2256]{4,0,3,2,1:T(8,128)} %slice.1086), channel_id=1, source_target_pairs={{1,0},{2,1},{3,2},{4,3},{5,4},{6,5},{7,6},{8,7},{9,8},{10,9},{11,1... | collective-permute-start | bytes 2598920 | tf_op jit(solution)/shard_map/ppermute | solution.py:17
  7.5 20.5 %collective-permute-start = (f32[8,2,3,2,2352]{4,0,3,2,1:T(8,128)}, f32[8,2,3,2,2352]{4,0,3,2,1:T(8,128)}, u32[]{:S(2)}, u32[]{:S(2)}) collective-permute-start(f32[8,2,3,2,2352]{4,0,3,2,1:T(8,128)} %pad_maximum_fusion.10), channel_id=1, source_target_pairs={{31,0},{0,1},{1,2},{2,3},{3,4},{4,5},{5,6},{6,7},{7,8},{8,9},{9,10... | collective-permute-start | bytes 2709512 | tf_op jit(solution)/shard_map/ppermute | solution.py:17
  12.0 27.8 %copy-start = (f32[8,2,3,2,3456]{4,0,3,2,1:T(8,128)}, f32[8,2,3,2,3456]{4,0,3,2,1:T(8,128)S(1)}, u32[]{:S(2)}) copy-start(f32[8,2,3,2,3456]{4,0,3,2,1:T(8,128)S(1)} %maximum_select_fusion) | copy-start | bytes 3981316
  12.0 18.1 %copy-start.91 = (f32[8,2,3,2,1200]{4,0,3,2,1:T(8,128)S(1)}, f32[8,2,3,2,1200]{4,0,3,2,1:T(8,128)}, u32[]{:S(2)}) copy-start(f32[8,2,3,2,1200]{4,0,3,2,1:T(8,128)} %slice.1085) | copy-start | bytes 1382404
  65.3 34.4 %all-to-all-start = ((f32[72,32,96]{2,0,1:T(8,128)}), f32[72,32,96]{2,0,1:T(8,128)}, u32[]{:S(2)}, u32[]{:S(2)}) async-start(f32[72,32,96]{2,0,1:T(8,128)} %copy.286), calls=%async_computation | async-start | bytes 2359296 | tf_op jit(solution)/shard_map/all_to_all | solution.py:217
  191.6 32.8 %all-to-all-start.1 = ((f32[32,72,96]{2,1,0:T(8,128)}), f32[32,72,96]{2,1,0:T(8,128)}, u32[]{:S(2)}, u32[]{:S(2)}) async-start(f32[32,72,96]{2,1,0:T(8,128)} %bitcast.4470), calls=%async_computation.1 | async-start | bytes 2359296 | tf_op jit(solution)/shard_map/all_to_all | solution.py:239
  243.0 14.2 %copy-start.29 = (f32[8,3456]{1,0:T(8,128)}, f32[8,3456]{1,0:T(8,128)S(1)}, u32[]{:S(2)}) copy-start(f32[8,3456]{1,0:T(8,128)S(1)} %get-tuple-element.199) | copy-start | bytes 331780
  243.1 14.2 %copy-start.32 = (f32[8,3456]{1,0:T(8,128)}, f32[8,3456]{1,0:T(8,128)S(1)}, u32[]{:S(2)}) copy-start(f32[8,3456]{1,0:T(8,128)S(1)} %get-tuple-element.200) | copy-start | bytes 331780
  243.1 14.2 %copy-start.35 = (f32[8,3456]{1,0:T(8,128)}, f32[8,3456]{1,0:T(8,128)S(1)}, u32[]{:S(2)}) copy-start(f32[8,3456]{1,0:T(8,128)S(1)} %get-tuple-element.201) | copy-start | bytes 331780
  243.1 14.2 %copy-start.38 = (f32[8,3456]{1,0:T(8,128)}, f32[8,3456]{1,0:T(8,128)S(1)}, u32[]{:S(2)}) copy-start(f32[8,3456]{1,0:T(8,128)S(1)} %get-tuple-element.203) | copy-start | bytes 331780
  252.0 32.0 %collective-permute-start.2 = (f32[3,3,2,8,2256]{4,3,2,1,0:T(8,128)S(1)}, f32[3,3,2,8,2256]{4,3,2,1,0:T(8,128)}, u32[]{:S(2)}, u32[]{:S(2)}) collective-permute-start(f32[3,3,2,8,2256]{4,3,2,1,0:T(8,128)S(1)} %slice.1270), channel_id=1, source_target_pairs={{31,0},{0,1},{1,2},{2,3},{3,4},{4,5},{5,6},{6,7},{7,8},{8,9},{9,10... | collective-permute-start | bytes 3898376 | tf_op jit(solution)/shard_map/ppermute | solution.py:17
  252.0 31.9 %collective-permute-start.3 = (f32[3,3,2,8,2304]{4,3,2,1,0:T(8,128)S(1)}, f32[3,3,2,8,2304]{4,3,2,1,0:T(8,128)}, u32[]{:S(2)}, u32[]{:S(2)}) collective-permute-start(f32[3,3,2,8,2304]{4,3,2,1,0:T(8,128)S(1)} %slice.1271), channel_id=1, source_target_pairs={{1,0},{2,1},{3,2},{4,3},{5,4},{6,5},{7,6},{8,7},{9,8},{10,9},{11,1... | collective-permute-start | bytes 3981320 | tf_op jit(solution)/shard_map/ppermute | solution.py:17
  296.7 31.8 %copy-start.69 = (f32[8,3456]{1,0:T(8,128)}, f32[8,3456]{1,0:T(8,128)S(1)}, u32[]{:S(2)}) copy-start(f32[8,3456]{1,0:T(8,128)S(1)} %get-tuple-element.21) | copy-start | bytes 331780
  296.7 31.8 %copy-start.71 = (f32[8,3456]{1,0:T(8,128)}, f32[8,3456]{1,0:T(8,128)S(1)}, u32[]{:S(2)}) copy-start(f32[8,3456]{1,0:T(8,128)S(1)} %get-tuple-element.22) | copy-start | bytes 331780
  296.7 31.8 %copy-start.73 = (f32[8,3456]{1,0:T(8,128)}, f32[8,3456]{1,0:T(8,128)S(1)}, u32[]{:S(2)}) copy-start(f32[8,3456]{1,0:T(8,128)S(1)} %get-tuple-element.23) | copy-start | bytes 331780
  296.7 31.8 %copy-start.75 = (f32[8,3456]{1,0:T(8,128)}, f32[8,3456]{1,0:T(8,128)S(1)}, u32[]{:S(2)}) copy-start(f32[8,3456]{1,0:T(8,128)S(1)} %get-tuple-element.24) | copy-start | bytes 331780
  296.7 31.8 %copy-start.77 = (f32[8,3456]{1,0:T(8,128)}, f32[8,3456]{1,0:T(8,128)S(1)}, u32[]{:S(2)}) copy-start(f32[8,3456]{1,0:T(8,128)S(1)} %get-tuple-element.26) | copy-start | bytes 331780
  296.7 31.8 %copy-start.79 = (f32[8,3456]{1,0:T(8,128)}, f32[8,3456]{1,0:T(8,128)S(1)}, u32[]{:S(2)}) copy-start(f32[8,3456]{1,0:T(8,128)S(1)} %get-tuple-element.44) | copy-start | bytes 331780
  296.7 31.8 %copy-start.81 = (f32[8,3456]{1,0:T(8,128)}, f32[8,3456]{1,0:T(8,128)S(1)}, u32[]{:S(2)}) copy-start(f32[8,3456]{1,0:T(8,128)S(1)} %get-tuple-element.45) | copy-start | bytes 331780
  296.7 31.8 %copy-start.83 = (f32[8,3456]{1,0:T(8,128)}, f32[8,3456]{1,0:T(8,128)S(1)}, u32[]{:S(2)}) copy-start(f32[8,3456]{1,0:T(8,128)S(1)} %get-tuple-element.46) | copy-start | bytes 331780
  296.7 31.8 %copy-start.85 = (f32[8,3456]{1,0:T(8,128)}, f32[8,3456]{1,0:T(8,128)S(1)}, u32[]{:S(2)}) copy-start(f32[8,3456]{1,0:T(8,128)S(1)} %get-tuple-element.47) | copy-start | bytes 331780
  296.7 31.8 %copy-start.87 = (f32[8,3456]{1,0:T(8,128)}, f32[8,3456]{1,0:T(8,128)S(1)}, u32[]{:S(2)}) copy-start(f32[8,3456]{1,0:T(8,128)S(1)} %get-tuple-element.48) | copy-start | bytes 331780
  296.7 31.8 %copy-start.89 = (f32[8,3456]{1,0:T(8,128)}, f32[8,3456]{1,0:T(8,128)S(1)}, u32[]{:S(2)}) copy-start(f32[8,3456]{1,0:T(8,128)S(1)} %get-tuple-element.49) | copy-start | bytes 331780
  296.8 31.8 %copy-start.92 = (f32[8,3456]{1,0:T(8,128)}, f32[8,3456]{1,0:T(8,128)S(1)}, u32[]{:S(2)}) copy-start(f32[8,3456]{1,0:T(8,128)S(1)} %get-tuple-element.25) | copy-start | bytes 331780
  (107 other events, 355.2 us)
where the time goes:
time: 415 us; the launch traced here: 409 us
  local copies, waits for them, and re-layouts  116 us (28%)
  waiting for transfers between devices  90.2 us (22%)
  other arithmetic  69.1 us (17%)
  matrix products  68.1 us (16%)
  blocking collectives  40.9 us (10%)
  starting transfers between devices  15.4 us (4%)
  between operations  9.56 us (2%)
    ppermute x4, waiting for transfers between devices, from_behind(): return lax.ppermute(block, axis, route)  41.5 us
    psum x1, blocking collectives, body(): theta_total = lax.psum(theta_part, ('tm', 'space'))  40.9 us
    dot_general x4, matrix products, plane_step(): with_sin = jnp.einsum(einsum_form, values, sine_table, precision=highest)  26.9 us
    all_to_all x1, waiting for transfers between devices, body(): lax.all_to_all(planes, 'space', split_axis=0, concat_axis=1, tiled=True)  25.8 us
    all_to_all x1, waiting for transfers between devices, body(): lax.all_to_all(packed, 'space', split_axis=1, concat_axis=0, tiled=True)  22.8 us
    dot_general x4, matrix products, plane_step(): with_cos = jnp.einsum(einsum_form, values, cosine_table, precision=highest)  21.5 us
    slice x30, local copies, waits for them, and re-layouts, body(): jnp.roll(a, extent - 1, axis=-1)  19.4 us
    slice x30, local copies, waits for them, and re-layouts, body(): jnp.roll(a, -1, axis=-1)  19.2 us
  transfers between devices with their start and end apart: 6, of which 4 were waited for; matrix products, arithmetic and copies ran while one was open for 4% of the time, Pallas kernels for 0%

commit v1 on v0

--- a/solution.py
+++ b/solution.py
@@ -236,7 +236,10 @@
     planes = plane_step(planes, "yzc,kz->ykc", cosine_table, sine_table, 1.0, pair_count)
     planes = plane_step(planes, "yzc,ky->kzc", cosine_table, sine_table, 1.0, pair_count)
     planes = jnp.roll(planes.reshape(plane_size, -1), storage_offset, axis=0)
-    returned = lax.all_to_all(planes, "space", split_axis=0, concat_axis=1, tiled=True)
+    returned = jnp.concatenate(
+        lax.all_to_all(jnp.stack(jnp.split(planes, lax.axis_size("space"), axis=0)), "space", 0, 0),
+        axis=1,
+    )
     returned = returned.reshape(rows_dev, 4, extent, 2, slices)
     real_back = returned[:, :, :, 0]
     imag_back = returned[:, :, :, 1]

time: 415 us -> 468 us (1.13)
  local copies, waits for them, and re-layouts: 116 us -> 168 us
    unnamed x256 -> x355, local copies, waits for them, and re-layouts: 9.81 us -> 58.5 us
where the time goes in v1:
time: 468 us; the launch traced here: 461 us
  local copies, waits for them, and re-layouts  168 us (36%)
  waiting for transfers between devices  90.1 us (19%)
  other arithmetic  68.1 us (15%)
  matrix products  68.1 us (15%)
  blocking collectives  40.9 us (9%)
  starting transfers between devices  15.4 us (3%)
  between operations  9.95 us (2%)
    unnamed x355, local copies, waits for them, and re-layouts  58.5 us
    ppermute x4, waiting for transfers between devices, from_behind(): return lax.ppermute(block, axis, route)  41.5 us
    psum x1, blocking collectives, body(): theta_total = lax.psum(theta_part, ('tm', 'space'))  40.9 us
    dot_general x4, matrix products, plane_step(): with_sin = jnp.einsum(einsum_form, values, sine_table, precision=highest)  27 us
    all_to_all x1, waiting for transfers between devices, body(): lax.all_to_all(jnp.stack(jnp.split(planes, lax.axis_size('space'), axis=0...  25.8 us
    all_to_all x1, waiting for transfers between devices, body(): lax.all_to_all(packed, 'space', split_axis=1, concat_axis=0, tiled=True)  22.8 us
    dot_general x4, matrix products, plane_step(): with_cos = jnp.einsum(einsum_form, values, cosine_table, precision=highest)  21.6 us
    slice x30, local copies, waits for them, and re-layouts, body(): jnp.roll(a, extent - 1, axis=-1)  19.3 us
  transfers between devices with their start and end apart: 6, of which 4 were waited for; matrix products, arithmetic and copies ran while one was open for 4% of the time, Pallas kernels for 0%

profile of v1, /device:TPU:12, one launch (start us, length us, event | category | flops | bytes accessed | tf_op | source)
XLA Modules:
  0.0 460.7 jit_solution(1600749404201885609)
XLA Ops:
  0.6 3.5 fusion.980
  12.1 16.0 %collective-permute-done = f32[8,2,3,2,2352]{4,0,3,2,1:T(8,128)} collective-permute-done((f32[8,2,3,2,2352]{4,0,3,2,1:T(8,128)}, f32[8,2,3,2,2352]{4,0,3,2,1:T(8,128)}, u32[]{:S(2)}, u32[]{:S(2)}) %collective-permute-start) | collective-permute-done | bytes 903200 | tf_op jit(solution)/shard_map/ppermute | solution.py:17
  40.9 3.7 reshape_reshape.12
  44.6 4.7 %fusion.9 = f32[48,4,8,72]{3,0,2,1:T(8,128)S(1)} fusion(f32[4,2,8,72,48]{4,3,2,1,0:T(8,128)} %reshape_reshape.12), kind=kOutput, calls=%fused_computation.66 | convolution fusion | flops 63721728 | bytes 1622016 | tf_op jit(solution)/shard_map/csqx,kx->qcks/dot_general | solution.py:214
  49.4 4.6 fusion.8
  54.0 3.3 fusion.2
  57.3 3.3 fusion.3
  65.3 6.9 %all-to-all-start = ((f32[72,32,96]{2,0,1:T(8,128)}), f32[72,32,96]{2,0,1:T(8,128)}, u32[]{:S(2)}, u32[]{:S(2)}) async-start(f32[72,32,96]{2,0,1:T(8,128)} %copy.342), calls=%async_computation | async-start | bytes 2359296 | tf_op jit(solution)/shard_map/all_to_all | solution.py:217
  76.9 22.8 %all-to-all-done = f32[72,32,96]{2,0,1:T(8,128)} async-done(((f32[72,32,96]{2,0,1:T(8,128)}), f32[72,32,96]{2,0,1:T(8,128)}, u32[]{:S(2)}, u32[]{:S(2)}) %all-to-all-start) | async-done | bytes 884768 | tf_op jit(solution)/shard_map/all_to_all | solution.py:217
  116.5 3.1 copy.351
  119.6 10.3 %fusion.729 = f32[48,48,6,2,8]{1,0,4,3,2:T(8,128)S(1)} fusion(f32[48,6,2,8,48]{4,0,3,2,1:T(8,128)} %bitcast.4520), kind=kOutput, calls=%fused_computation.1675 | convolution fusion | flops 127422720 | bytes 1769472 | tf_op jit(solution)/shard_map/yzc,ky->kzc/dot_general | solution.py:154
  129.9 8.5 %fusion.739 = f32[48,48,6,2,8]{1,0,4,3,2:T(8,128)S(1)} fusion(f32[48,6,2,8,48]{4,0,3,2,1:T(8,128)S(1)} %bitcast.4521), kind=kOutput, calls=%fused_computation.1685 | convolution fusion | flops 127422720 | bytes 1769472 | tf_op jit(solution)/shard_map/yzc,ky->kzc/dot_general | solution.py:153
  140.3 3.2 copy.355
  143.6 4.1 convolution_bitcast_fusion
  159.9 3.3 copy.361
  163.2 10.3 %fusion.727 = f32[48,48,6,2,8]{1,0,4,3,2:T(8,128)S(1)} fusion(f32[48,6,2,8,48]{4,0,3,2,1:T(8,128)} %bitcast.4522), kind=kOutput, calls=%fused_computation.1673 | convolution fusion | flops 127422720 | bytes 1769472 | tf_op jit(solution)/shard_map/yzc,ky->kzc/dot_general | solution.py:154
  173.5 8.5 %fusion.741 = f32[48,48,6,2,8]{1,0,4,3,2:T(8,128)S(1)} fusion(f32[48,6,2,8,48]{4,0,3,2,1:T(8,128)S(1)} %bitcast.4523), kind=kOutput, calls=%fused_computation.1687 | convolution fusion | flops 127422720 | bytes 1769472 | tf_op jit(solution)/shard_map/yzc,ky->kzc/dot_general | solution.py:153
  242.9 5.0 %all-to-all-start.1 = ((f32[32,72,96]{2,1,0:T(8,128)}), f32[32,72,96]{2,1,0:T(8,128)}, u32[]{:S(2)}, u32[]{:S(2)}) async-start(f32[32,72,96]{2,1,0:T(8,128)} %constant_dynamic-update-slice_fusion), calls=%async_computation.1 | async-start | bytes 2359296 | tf_op jit(solution)/shard_map/all_to_all | solution.py:240
  249.8 25.8 %all-to-all-done.1 = f32[32,72,96]{2,1,0:T(8,128)} async-done(((f32[32,72,96]{2,1,0:T(8,128)}), f32[32,72,96]{2,1,0:T(8,128)}, u32[]{:S(2)}, u32[]{:S(2)}) %all-to-all-start.1) | async-done | bytes 884768 | tf_op jit(solution)/shard_map/all_to_all | solution.py:240
  309.8 25.6 %collective-permute-done.2 = f32[3,3,2,8,2256]{4,3,2,1,0:T(8,128)} collective-permute-done((f32[3,3,2,8,2256]{4,3,2,1,0:T(8,128)S(1)}, f32[3,3,2,8,2256]{4,3,2,1,0:T(8,128)}, u32[]{:S(2)}, u32[]{:S(2)}) %collective-permute-start.2) | collective-permute-done | bytes 1299488 | tf_op jit(solution)/shard_map/ppermute | solution.py:17
  335.3 6.6 %concatenate.1157 = f32[3,3,2,8,8016]{4,3,2,1,0:T(8,128)} concatenate(f32[3,3,2,8,2256]{4,3,2,1,0:T(8,128)} %collective-permute-done.2, f32[3,3,2,8,3456]{4,3,2,1,0:T(8,128)} %copy-done.7, f32[3,3,2,8,2304]{4,3,2,1,0:T(8,128)} %collective-permute-done.3), dimensions={4} | concatenate | bytes 9234432 | tf_op jit(solution)/shard_map/concatenate | solution.py:259
  409.2 3.4 fusion.708
  413.2 4.0 copy.419
  417.2 40.9 %all-reduce = (f32[]{:T(128)}, f32[8]{0:T(128)S(1)}) all-reduce(f32[]{:T(128)S(6)} %add.9190, f32[8]{0:T(128)S(1)} %add_add_fusion.11), channel_id=1, replica_groups=mesh['tm'=1,'space'=32] {'tm','space'}, use_global_device_ids=true, to_apply=%region_8.9 | all-reduce | flops 9 | bytes 72 | tf_op jit(solution)/shard_map/psum | solution.py:198
  (568 shorter events, 219.5 us)
Async XLA Ops:
  5.2 24.8 %collective-permute-start.1 = (f32[8,2,3,2,2256]{4,0,3,2,1:T(8,128)}, f32[8,2,3,2,2256]{4,0,3,2,1:T(8,128)}, u32[]{:S(2)}, u32[]{:S(2)}) collective-permute-start(f32[8,2,3,2,2256]{4,0,3,2,1:T(8,128)} %slice.1148), channel_id=1, source_target_pairs={{1,0},{2,1},{3,2},{4,3},{5,4},{6,5},{7,6},{8,7},{9,8},{10,9},{11,1... | collective-permute-start | bytes 2598920 | tf_op jit(solution)/shard_map/ppermute | solution.py:17
  7.5 20.5 %collective-permute-start = (f32[8,2,3,2,2352]{4,0,3,2,1:T(8,128)}, f32[8,2,3,2,2352]{4,0,3,2,1:T(8,128)}, u32[]{:S(2)}, u32[]{:S(2)}) collective-permute-start(f32[8,2,3,2,2352]{4,0,3,2,1:T(8,128)} %pad_maximum_fusion.9), channel_id=1, source_target_pairs={{31,0},{0,1},{1,2},{2,3},{3,4},{4,5},{5,6},{6,7},{7,8},{8,9},{9,10... | collective-permute-start | bytes 2709512 | tf_op jit(solution)/shard_map/ppermute | solution.py:17
  12.0 27.8 %copy-start = (f32[8,2,3,2,3456]{4,0,3,2,1:T(8,128)}, f32[8,2,3,2,3456]{4,0,3,2,1:T(8,128)S(1)}, u32[]{:S(2)}) copy-start(f32[8,2,3,2,3456]{4,0,3,2,1:T(8,128)S(1)} %maximum_select_fusion) | copy-start | bytes 3981316
  65.3 34.4 %all-to-all-start = ((f32[72,32,96]{2,0,1:T(8,128)}), f32[72,32,96]{2,0,1:T(8,128)}, u32[]{:S(2)}, u32[]{:S(2)}) async-start(f32[72,32,96]{2,0,1:T(8,128)} %copy.342), calls=%async_computation | async-start | bytes 2359296 | tf_op jit(solution)/shard_map/all_to_all | solution.py:217
  191.0 23.2 %copy-start.129 = (f32[72,96]{0,1:T(8,128)S(1)}, f32[72,96]{0,1:T(8,128)}, u32[]{:S(2)}) copy-start(f32[72,96]{0,1:T(8,128)} %get-tuple-element.301) | copy-start | bytes 82948
  191.0 23.3 %copy-start.128 = (f32[72,96]{0,1:T(8,128)S(1)}, f32[72,96]{0,1:T(8,128)}, u32[]{:S(2)}) copy-start(f32[72,96]{0,1:T(8,128)} %get-tuple-element.300) | copy-start | bytes 82948
  191.0 23.3 %copy-start.127 = (f32[72,96]{0,1:T(8,128)S(1)}, f32[72,96]{0,1:T(8,128)}, u32[]{:S(2)}) copy-start(f32[72,96]{0,1:T(8,128)} %get-tuple-element.299) | copy-start | bytes 82948
  191.0 23.4 %copy-start.126 = (f32[72,96]{0,1:T(8,128)S(1)}, f32[72,96]{0,1:T(8,128)}, u32[]{:S(2)}) copy-start(f32[72,96]{0,1:T(8,128)} %get-tuple-element.298) | copy-start | bytes 82948
  191.0 23.5 %copy-start.125 = (f32[72,96]{0,1:T(8,128)S(1)}, f32[72,96]{0,1:T(8,128)}, u32[]{:S(2)}) copy-start(f32[72,96]{0,1:T(8,128)} %get-tuple-element.297) | copy-start | bytes 82948
  242.9 32.8 %all-to-all-start.1 = ((f32[32,72,96]{2,1,0:T(8,128)}), f32[32,72,96]{2,1,0:T(8,128)}, u32[]{:S(2)}, u32[]{:S(2)}) async-start(f32[32,72,96]{2,1,0:T(8,128)} %constant_dynamic-update-slice_fusion), calls=%async_computation.1 | async-start | bytes 2359296 | tf_op jit(solution)/shard_map/all_to_all | solution.py:240
  303.4 32.0 %collective-permute-start.2 = (f32[3,3,2,8,2256]{4,3,2,1,0:T(8,128)S(1)}, f32[3,3,2,8,2256]{4,3,2,1,0:T(8,128)}, u32[]{:S(2)}, u32[]{:S(2)}) collective-permute-start(f32[3,3,2,8,2256]{4,3,2,1,0:T(8,128)S(1)} %slice.1332), channel_id=1, source_target_pairs={{31,0},{0,1},{1,2},{2,3},{3,4},{4,5},{5,6},{6,7},{7,8},{8,9},{9,10... | collective-permute-start | bytes 3898376 | tf_op jit(solution)/shard_map/ppermute | solution.py:17
  303.4 31.9 %collective-permute-start.3 = (f32[3,3,2,8,2304]{4,3,2,1,0:T(8,128)S(1)}, f32[3,3,2,8,2304]{4,3,2,1,0:T(8,128)}, u32[]{:S(2)}, u32[]{:S(2)}) collective-permute-start(f32[3,3,2,8,2304]{4,3,2,1,0:T(8,128)S(1)} %slice.1333), channel_id=1, source_target_pairs={{1,0},{2,1},{3,2},{4,3},{5,4},{6,5},{7,6},{8,7},{9,8},{10,9},{11,1... | collective-permute-start | bytes 3981320 | tf_op jit(solution)/shard_map/ppermute | solution.py:17
  348.1 31.8 %copy-start.69 = (f32[8,3456]{1,0:T(8,128)}, f32[8,3456]{1,0:T(8,128)S(1)}, u32[]{:S(2)}) copy-start(f32[8,3456]{1,0:T(8,128)S(1)} %get-tuple-element.21) | copy-start | bytes 331780
  348.1 31.8 %copy-start.71 = (f32[8,3456]{1,0:T(8,128)}, f32[8,3456]{1,0:T(8,128)S(1)}, u32[]{:S(2)}) copy-start(f32[8,3456]{1,0:T(8,128)S(1)} %get-tuple-element.22) | copy-start | bytes 331780
  348.1 31.8 %copy-start.73 = (f32[8,3456]{1,0:T(8,128)}, f32[8,3456]{1,0:T(8,128)S(1)}, u32[]{:S(2)}) copy-start(f32[8,3456]{1,0:T(8,128)S(1)} %get-tuple-element.23) | copy-start | bytes 331780
  348.1 31.8 %copy-start.75 = (f32[8,3456]{1,0:T(8,128)}, f32[8,3456]{1,0:T(8,128)S(1)}, u32[]{:S(2)}) copy-start(f32[8,3456]{1,0:T(8,128)S(1)} %get-tuple-element.24) | copy-start | bytes 331780
  348.1 31.8 %copy-start.77 = (f32[8,3456]{1,0:T(8,128)}, f32[8,3456]{1,0:T(8,128)S(1)}, u32[]{:S(2)}) copy-start(f32[8,3456]{1,0:T(8,128)S(1)} %get-tuple-element.26) | copy-start | bytes 331780
  348.1 31.8 %copy-start.79 = (f32[8,3456]{1,0:T(8,128)}, f32[8,3456]{1,0:T(8,128)S(1)}, u32[]{:S(2)}) copy-start(f32[8,3456]{1,0:T(8,128)S(1)} %get-tuple-element.44) | copy-start | bytes 331780
  348.1 31.8 %copy-start.81 = (f32[8,3456]{1,0:T(8,128)}, f32[8,3456]{1,0:T(8,128)S(1)}, u32[]{:S(2)}) copy-start(f32[8,3456]{1,0:T(8,128)S(1)} %get-tuple-element.45) | copy-start | bytes 331780
  348.2 31.8 %copy-start.83 = (f32[8,3456]{1,0:T(8,128)}, f32[8,3456]{1,0:T(8,128)S(1)}, u32[]{:S(2)}) copy-start(f32[8,3456]{1,0:T(8,128)S(1)} %get-tuple-element.46) | copy-start | bytes 331780
  348.2 31.8 %copy-start.85 = (f32[8,3456]{1,0:T(8,128)}, f32[8,3456]{1,0:T(8,128)S(1)}, u32[]{:S(2)}) copy-start(f32[8,3456]{1,0:T(8,128)S(1)} %get-tuple-element.47) | copy-start | bytes 331780
  348.2 31.8 %copy-start.87 = (f32[8,3456]{1,0:T(8,128)}, f32[8,3456]{1,0:T(8,128)S(1)}, u32[]{:S(2)}) copy-start(f32[8,3456]{1,0:T(8,128)S(1)} %get-tuple-element.48) | copy-start | bytes 331780
  348.2 31.8 %copy-start.89 = (f32[8,3456]{1,0:T(8,128)}, f32[8,3456]{1,0:T(8,128)S(1)}, u32[]{:S(2)}) copy-start(f32[8,3456]{1,0:T(8,128)S(1)} %get-tuple-element.49) | copy-start | bytes 331780
  348.2 31.8 %copy-start.92 = (f32[8,3456]{1,0:T(8,128)}, f32[8,3456]{1,0:T(8,128)S(1)}, u32[]{:S(2)}) copy-start(f32[8,3456]{1,0:T(8,128)S(1)} %get-tuple-element.25) | copy-start | bytes 331780
  (126 other events, 694.8 us)
